TPU v7x, 32 devices: a whole 2x2x4 slice. The times are simulated.
32 devices in a mesh: grp: 4 (over y, core), blk: 8 (over z, x).
Axes of the slice: x: 2, y: 2, z: 4, core: 2. Of those that a mesh axis runs over, the one named last changes fastest.
Arguments:
- queries: bfloat16 [4, 128, 4096], P(None, ('blk', 'grp')), may hold values from -24 to 24
- cache_keys: bfloat16 [4, 3584, 512], P('grp', 'blk'), may hold values from -24 to 24
- cache_values: bfloat16 [4, 3584, 512], P('grp', 'blk'), may hold values from -15 to 15
- new_keys: bfloat16 [4, 128, 512], P(None, ('blk', 'grp')), may hold values from -6 to 6
- new_values: bfloat16 [4, 128, 512], P(None, ('blk', 'grp')), may hold values from -15 to 15
- hits: int32 [4], P('grp'), may hold values from 448 to 3584, as said below
- counts: int32 [4], P('grp'), may hold values from 64 to 128, as said below
- assign: int32 [4, 8], P('grp'), may hold values from 0 to 7, each once within a row
Outputs:
- attended: bfloat16 [4, 128, 4096], P(None, ('blk', 'grp'))
Inputs may be any that keep to these rules, and one draw needn't show every extreme that they name: Cached positions of request r below hits[r] are valid; in every draw some request has all 3584 valid. New tokens of request r at order counts[r] or later are padding; in every draw some request has all 128.
All inputs are finite; a program needn't handle non-finite values.
Results may differ from a plain program's by a relative error of at most 0.0085.
Values may be sent and summed in bfloat16 or wider, within the bound.
A program may use at most 128 MiB of HBM per device.

v0:
```python
import jax
import jax.numpy as jnp
from jax import lax
from jax.sharding import PartitionSpec as P

HEAD_DIM = 128


def shifted(value, axis, by):
    length = lax.axis_size(axis)
    return lax.ppermute(value, axis, [(i, (i + by) % length) for i in range(length)])


def partial_block(queries, keys, values, allowed, kv_heads):
    row_count, full_width = queries.shape
    key_count = keys.shape[0]
    head_dim = keys.shape[1] // kv_heads
    group_size = full_width // head_dim // kv_heads
    query_heads = queries.reshape(row_count, kv_heads, group_size, head_dim)
    key_heads = keys.reshape(key_count, kv_heads, head_dim)
    scores = jnp.einsum(
        "qkgd,nkd->kgqn", query_heads, key_heads, preferred_element_type=jnp.float32
    ) * head_dim ** (-0.5)
    scores = jnp.where(allowed[None, None], scores, -1e30)
    block_max = jnp.max(scores, axis=-1)
    exp_terms = jnp.where(allowed[None, None], jnp.exp(scores - block_max[..., None]), 0.0)
    weight_sum = jnp.sum(exp_terms, axis=-1)
    prob_bf = exp_terms.astype(jnp.bfloat16)
    value_heads = values.reshape(key_count, kv_heads, head_dim)
    blended = jnp.einsum("kgqn,nkd->qkgd", prob_bf, value_heads, preferred_element_type=jnp.float32)
    floor_sum = jnp.maximum(weight_sum, 1.0).transpose(2, 0, 1)[..., None]
    blended = (blended / floor_sum).reshape(row_count, full_width).astype(jnp.bfloat16)
    maxima = block_max.transpose(2, 0, 1).reshape(row_count, -1)
    weights = weight_sum.transpose(2, 0, 1).reshape(row_count, -1)
    return (blended, maxima, weights)


def combine(running, part, head_count):
    summed, maxima, weights = running
    blended, part_max, part_weight = part
    row_count, full_width = summed.shape
    highest = jnp.maximum(maxima, part_max)
    old_scale = jnp.exp(maxima - highest)
    new_scale = part_weight * jnp.exp(part_max - highest)
    summed = summed.reshape(row_count, head_count, -1) * old_scale[:, :, None]
    summed = summed + new_scale[:, :, None] * blended.astype(jnp.float32).reshape(
        row_count, head_count, -1
    )
    return (summed.reshape(row_count, full_width), highest, weights * old_scale + new_scale)


def local(queries, cache_keys, cache_values, new_keys, new_values, hits, counts, assign):
    local_q, local_k, local_v = (
        lax.all_to_all(queries, "grp", split_axis=0, concat_axis=1, tiled=True),
        lax.all_to_all(new_keys, "grp", split_axis=0, concat_axis=1, tiled=True),
        lax.all_to_all(new_values, "grp", split_axis=0, concat_axis=1, tiled=True),
    )
    local_q = local_q[0]
    local_k = local_k[0]
    local_v = local_v[0]
    row_count, full_width = local_q.shape
    kv_width = local_k.shape[1]
    cached = cache_keys.shape[1]
    head_count = full_width // HEAD_DIM
    kv_heads = kv_width // HEAD_DIM
    hit_limit = hits[0]
    filled = counts[0]
    block_order = assign[0]
    cycle_index = lax.axis_index("blk")
    members = lax.axis_size("blk")
    query_lane = jnp.arange(row_count, dtype=jnp.int32)
    cache_lane = jnp.arange(cached, dtype=jnp.int32)
    own_pos = block_order[cycle_index] * row_count + query_lane
    block_keys = jnp.concatenate([cache_keys[0], local_k], 0)
    block_values = jnp.concatenate([cache_values[0], local_v], 0)

    def allowed_for(block_index, query_pos):
        cache_ok = block_index * cached + cache_lane < hit_limit
        fresh_ok = (block_order[block_index] * row_count + query_lane)[None, :] <= query_pos[
            :, None
        ]
        return jnp.concatenate(
            [jnp.broadcast_to(cache_ok[None, :], (query_pos.shape[0], cached)), fresh_ok], 1
        )

    start = (
        jnp.zeros((row_count, full_width), jnp.float32),
        jnp.full((row_count, head_count), -1e30, jnp.float32),
        jnp.zeros((row_count, head_count), jnp.float32),
    )

    def pass_state(running):
        return shifted(running, "blk", 1)

    def visit_block(visitor, running, turn_index):
        source = (cycle_index - turn_index) % members
        query_pos = block_order[source] * row_count + query_lane
        part = partial_block(
            visitor, block_keys, block_values, allowed_for(cycle_index, query_pos), kv_heads
        )
        return pass_state(combine(running, part, head_count))

    def cycle_turn(turn_index, loop_state):
        visitor, running = loop_state
        running = visit_block(visitor, running, turn_index)
        visitor = shifted(visitor, "blk", 1)
        return (visitor, running)

    visitor, running = lax.fori_loop(0, members - 1, cycle_turn, (local_q, start))
    running = visit_block(visitor, running, members - 1)
    summed, maxima, weights = running
    blended = (summed.reshape(row_count, head_count, -1) / weights[:, :, None]).reshape(
        row_count, full_width
    )
    blended = jnp.where((own_pos < filled)[:, None], blended, 0.0).astype(jnp.bfloat16)
    return lax.all_to_all(blended[None], "grp", split_axis=1, concat_axis=0, tiled=True)


def solution(mesh):
    return jax.shard_map(
        local,
        mesh=mesh,
        in_specs=(
            P(None, ("blk", "grp"), None),
            P("grp", "blk", None),
            P("grp", "blk", None),
            P(None, ("blk", "grp"), None),
            P(None, ("blk", "grp"), None),
            P("grp"),
            P("grp"),
            P("grp", None),
        ),
        out_specs=P(None, ("blk", "grp"), None),
        check_vma=False,
    )
```

profile of v0, /device:TPU:0, one launch (start us, length us, event | category | flops | bytes accessed | tf_op | source)
XLA Modules:
  0.0 164.6 jit_solution(10242938498501873092)
XLA Ops:
  0.0 4.3 %all-to-all-start.1 = ((bf16[4,4,512]{2,1,0:T(4,128)(2,1)}), bf16[4,4,512]{2,1,0:T(4,128)(2,1)S(1)}, u32[]{:S(2)}, u32[]{:S(2)}) async-start(bf16[4,4,512]{2,1,0:T(4,128)(2,1)} %param.13), calls=%async_computation.1 | async-start | bytes 32768 | tf_op jit(solution)/shard_map/all_to_all | solution.py:55
  10.0 3.4 %all-to-all-start.2 = ((bf16[4,4,512]{2,1,0:T(4,128)(2,1)}), bf16[4,4,512]{2,1,0:T(4,128)(2,1)S(1)}, u32[]{:S(2)}, u32[]{:S(2)}) async-start(bf16[4,4,512]{2,1,0:T(4,128)(2,1)} %param.14), calls=%async_computation.2 | async-start | bytes 32768 | tf_op jit(solution)/shard_map/all_to_all | solution.py:56
  13.7 3.7 %all-to-all-done.2 = bf16[4,4,512]{2,1,0:T(4,128)(2,1)S(1)} async-done(((bf16[4,4,512]{2,1,0:T(4,128)(2,1)}), bf16[4,4,512]{2,1,0:T(4,128)(2,1)S(1)}, u32[]{:S(2)}, u32[]{:S(2)}) %all-to-all-start.2) | async-done | bytes 16416 | tf_op jit(solution)/shard_map/all_to_all | solution.py:56
  17.3 3.3 %all-to-all-start = ((bf16[4,4,4096]{2,1,0:T(4,128)(2,1)}), bf16[4,4,4096]{2,1,0:T(4,128)(2,1)S(1)}, u32[]{:S(2)}, u32[]{:S(2)}) async-start(bf16[4,4,4096]{2,1,0:T(4,128)(2,1)} %param.10), calls=%async_computation | async-start | bytes 262144 | tf_op jit(solution)/shard_map/all_to_all | solution.py:54
  21.6 3.7 %all-to-all-done = bf16[4,4,4096]{2,1,0:T(4,128)(2,1)S(1)} async-done(((bf16[4,4,4096]{2,1,0:T(4,128)(2,1)}), bf16[4,4,4096]{2,1,0:T(4,128)(2,1)S(1)}, u32[]{:S(2)}, u32[]{:S(2)}) %all-to-all-start) | async-done | bytes 131104 | tf_op jit(solution)/shard_map/all_to_all | solution.py:54
  25.3 115.3 %while.24 = (s32[]{:T(128)}, bf16[16,4096]{1,0:T(8,128)(2,1)S(1)}, f32[16,4096]{1,0:T(8,128)S(1)}, f32[16,32]{0,1:T(8,128)S(1)}, f32[16,32]{0,1:T(8,128)S(1)}, /...) while((s32[]{:T(128)}, bf16[16,4096]{1,0:T(8,128)(2,1)S(1)}, ...), condition=%wide.wide.region_3.4_spmd.clone.clone, body=%wide.wide.region_0.3_spmd.clone.clone.sunk | while | flops 124177328 | bytes 8742969 | solution.py:109
  29.7 2.0 %collective-permute-start.1 = (f32[16,4096]{1,0:T(8,128)S(1)}, f32[16,4096]{1,0:T(8,128)S(1)}, u32[]{:S(2)}, u32[]{:S(2)}) collective-permute-start(f32[16,4096]{1,0:T(8,128)S(1)} %fusion.72), channel_id=1, source_target_pairs={{0,1},{1,2},{2,3},{3,4},{4,5},{5,6},{6,7},{7,0},{8,9},{9,10},{10,1... | collective-permute-start | bytes 786440 | tf_op jit(solution)/shard_map/while/body/eval_jaxpr/ppermute | solution.py:11
  31.7 1.5 collective-permute-start
  33.3 1.5 collective-permute-start.2
  34.8 1.5 collective-permute-start.3
  36.3 7.7 %collective-permute-done.2 = f32[16,32]{0,1:T(8,128)S(1)} collective-permute-done((f32[16,32]{0,1:T(8,128)S(1)}, f32[16,32]{0,1:T(8,128)S(1)}, u32[]{:S(2)}, u32[]{:S(2)}) %collective-permute-start.2) | collective-permute-done | bytes 2080 | tf_op jit(solution)/shard_map/while/body/eval_jaxpr/ppermute | solution.py:11
  50.4 2.5 %collective-permute-start.3 = (f32[16,32]{0,1:T(8,128)S(1)}, f32[16,32]{0,1:T(8,128)S(1)}, u32[]{:S(2)}, u32[]{:S(2)}) collective-permute-start(f32[16,32]{0,1:T(8,128)S(1)} %get-tuple-element.565), channel_id=1, source_target_pairs={{0,1},{1,2},{2,3},{3,4},{4,5},{5,6},{6,7},{7,0},{8,9},{9,10},{10,1... | collective-permute-start | bytes 6152 | tf_op jit(solution)/shard_map/while/body/eval_jaxpr/ppermute | solution.py:11
  52.8 8.9 %collective-permute-done.2 = f32[16,32]{0,1:T(8,128)S(1)} collective-permute-done((f32[16,32]{0,1:T(8,128)S(1)}, f32[16,32]{0,1:T(8,128)S(1)}, u32[]{:S(2)}, u32[]{:S(2)}) %collective-permute-start.2) | collective-permute-done | bytes 2080 | tf_op jit(solution)/shard_map/while/body/eval_jaxpr/ppermute | solution.py:11
  66.5 2.0 %collective-permute-start.3 = (f32[16,32]{0,1:T(8,128)S(1)}, f32[16,32]{0,1:T(8,128)S(1)}, u32[]{:S(2)}, u32[]{:S(2)}) collective-permute-start(f32[16,32]{0,1:T(8,128)S(1)} %get-tuple-element.565), channel_id=1, source_target_pairs={{0,1},{1,2},{2,3},{3,4},{4,5},{5,6},{6,7},{7,0},{8,9},{9,10},{10,1... | collective-permute-start | bytes 6152 | tf_op jit(solution)/shard_map/while/body/eval_jaxpr/ppermute | solution.py:11
  68.5 10.2 %collective-permute-done.2 = f32[16,32]{0,1:T(8,128)S(1)} collective-permute-done((f32[16,32]{0,1:T(8,128)S(1)}, f32[16,32]{0,1:T(8,128)S(1)}, u32[]{:S(2)}, u32[]{:S(2)}) %collective-permute-start.2) | collective-permute-done | bytes 2080 | tf_op jit(solution)/shard_map/while/body/eval_jaxpr/ppermute | solution.py:11
  83.5 11.2 %collective-permute-done.2 = f32[16,32]{0,1:T(8,128)S(1)} collective-permute-done((f32[16,32]{0,1:T(8,128)S(1)}, f32[16,32]{0,1:T(8,128)S(1)}, u32[]{:S(2)}, u32[]{:S(2)}) %collective-permute-start.2) | collective-permute-done | bytes 2080 | tf_op jit(solution)/shard_map/while/body/eval_jaxpr/ppermute | solution.py:11
  100.0 10.0 %collective-permute-done.2 = f32[16,32]{0,1:T(8,128)S(1)} collective-permute-done((f32[16,32]{0,1:T(8,128)S(1)}, f32[16,32]{0,1:T(8,128)S(1)}, u32[]{:S(2)}, u32[]{:S(2)}) %collective-permute-start.2) | collective-permute-done | bytes 2080 | tf_op jit(solution)/shard_map/while/body/eval_jaxpr/ppermute | solution.py:11
  114.7 1.3 collective-permute-start.3
  116.0 9.2 %collective-permute-done.2 = f32[16,32]{0,1:T(8,128)S(1)} collective-permute-done((f32[16,32]{0,1:T(8,128)S(1)}, f32[16,32]{0,1:T(8,128)S(1)}, u32[]{:S(2)}, u32[]{:S(2)}) %collective-permute-start.2) | collective-permute-done | bytes 2080 | tf_op jit(solution)/shard_map/while/body/eval_jaxpr/ppermute | solution.py:11
  130.0 1.3 collective-permute-start.3
  131.3 9.2 %collective-permute-done.2 = f32[16,32]{0,1:T(8,128)S(1)} collective-permute-done((f32[16,32]{0,1:T(8,128)S(1)}, f32[16,32]{0,1:T(8,128)S(1)}, u32[]{:S(2)}, u32[]{:S(2)}) %collective-permute-start.2) | collective-permute-done | bytes 2080 | tf_op jit(solution)/shard_map/while/body/eval_jaxpr/ppermute | solution.py:11
  143.7 8.5 %collective-permute-done.5 = f32[16,32]{0,1:T(8,128)S(1)} collective-permute-done((f32[16,32]{0,1:T(8,128)S(1)}, f32[16,32]{0,1:T(8,128)S(1)}, u32[]{:S(2)}, u32[]{:S(2)}) %collective-permute-start.5) | collective-permute-done | bytes 2080 | tf_op jit(solution)/shard_map/ppermute | solution.py:11
  153.3 1.4 reduce.2
  154.9 8.2 %all_to_all.19 = bf16[4,2,8192]{2,1,0:T(2,128)(2,1)S(1)} all-to-all(bf16[4,2,8192]{2,1,0:T(2,128)(2,1)S(1)} %reshape.215), channel_id=1, replica_groups=mesh['grp'=4,'blk'=8] {'grp'}, dimensions={0} | all-to-all | bytes 262144 | tf_op jit(solution)/shard_map/all_to_all | solution.py:116
  (243 shorter events, 39.8 us)
Async XLA Ops:
  29.7 14.5 %collective-permute-start.1 = (f32[16,4096]{1,0:T(8,128)S(1)}, f32[16,4096]{1,0:T(8,128)S(1)}, u32[]{:S(2)}, u32[]{:S(2)}) collective-permute-start(f32[16,4096]{1,0:T(8,128)S(1)} %fusion.72), channel_id=1, source_target_pairs={{0,1},{1,2},{2,3},{3,4},{4,5},{5,6},{6,7},{7,0},{8,9},{9,10},{10,1... | collective-permute-start | bytes 786440 | tf_op jit(solution)/shard_map/while/body/eval_jaxpr/ppermute | solution.py:11
  31.7 12.5 %collective-permute-start = (bf16[16,4096]{1,0:T(8,128)(2,1)S(1)}, bf16[16,4096]{1,0:T(8,128)(2,1)S(1)}, u32[]{:S(2)}, u32[]{:S(2)}) collective-permute-start(bf16[16,4096]{1,0:T(8,128)(2,1)S(1)} %copy.144), channel_id=1, source_target_pairs={{0,1},{1,2},{2,3},{3,4},{4,5},{5,6},{6,7},{7,0},{8,9},{9,10},{10,1... | collective-permute-start | bytes 393224 | tf_op jit(solution)/shard_map/while/body/eval_jaxpr/ppermute | solution.py:11
  33.3 10.8 %collective-permute-start.2 = (f32[16,32]{0,1:T(8,128)S(1)}, f32[16,32]{0,1:T(8,128)S(1)}, u32[]{:S(2)}, u32[]{:S(2)}) collective-permute-start(f32[16,32]{0,1:T(8,128)S(1)} %get-tuple-element.564), channel_id=1, source_target_pairs={{0,1},{1,2},{2,3},{3,4},{4,5},{5,6},{6,7},{7,0},{8,9},{9,10},{10,1... | collective-permute-start | bytes 6152 | tf_op jit(solution)/shard_map/while/body/eval_jaxpr/ppermute | solution.py:11
  48.6 13.4 %collective-permute-start.1 = (f32[16,4096]{1,0:T(8,128)S(1)}, f32[16,4096]{1,0:T(8,128)S(1)}, u32[]{:S(2)}, u32[]{:S(2)}) collective-permute-start(f32[16,4096]{1,0:T(8,128)S(1)} %fusion.72), channel_id=1, source_target_pairs={{0,1},{1,2},{2,3},{3,4},{4,5},{5,6},{6,7},{7,0},{8,9},{9,10},{10,1... | collective-permute-start | bytes 786440 | tf_op jit(solution)/shard_map/while/body/eval_jaxpr/ppermute | solution.py:11
  48.7 13.3 %collective-permute-start = (bf16[16,4096]{1,0:T(8,128)(2,1)S(1)}, bf16[16,4096]{1,0:T(8,128)(2,1)S(1)}, u32[]{:S(2)}, u32[]{:S(2)}) collective-permute-start(bf16[16,4096]{1,0:T(8,128)(2,1)S(1)} %copy.144), channel_id=1, source_target_pairs={{0,1},{1,2},{2,3},{3,4},{4,5},{5,6},{6,7},{7,0},{8,9},{9,10},{10,1... | collective-permute-start | bytes 393224 | tf_op jit(solution)/shard_map/while/body/eval_jaxpr/ppermute | solution.py:11
  49.8 12.0 %collective-permute-start.2 = (f32[16,32]{0,1:T(8,128)S(1)}, f32[16,32]{0,1:T(8,128)S(1)}, u32[]{:S(2)}, u32[]{:S(2)}) collective-permute-start(f32[16,32]{0,1:T(8,128)S(1)} %get-tuple-element.564), channel_id=1, source_target_pairs={{0,1},{1,2},{2,3},{3,4},{4,5},{5,6},{6,7},{7,0},{8,9},{9,10},{10,1... | collective-permute-start | bytes 6152 | tf_op jit(solution)/shard_map/while/body/eval_jaxpr/ppermute | solution.py:11
  50.4 11.6 %collective-permute-start.3 = (f32[16,32]{0,1:T(8,128)S(1)}, f32[16,32]{0,1:T(8,128)S(1)}, u32[]{:S(2)}, u32[]{:S(2)}) collective-permute-start(f32[16,32]{0,1:T(8,128)S(1)} %get-tuple-element.565), channel_id=1, source_target_pairs={{0,1},{1,2},{2,3},{3,4},{4,5},{5,6},{6,7},{7,0},{8,9},{9,10},{10,1... | collective-permute-start | bytes 6152 | tf_op jit(solution)/shard_map/while/body/eval_jaxpr/ppermute | solution.py:11
  66.3 12.5 %collective-permute-start.1 = (f32[16,4096]{1,0:T(8,128)S(1)}, f32[16,4096]{1,0:T(8,128)S(1)}, u32[]{:S(2)}, u32[]{:S(2)}) collective-permute-start(f32[16,4096]{1,0:T(8,128)S(1)} %fusion.72), channel_id=1, source_target_pairs={{0,1},{1,2},{2,3},{3,4},{4,5},{5,6},{6,7},{7,0},{8,9},{9,10},{10,1... | collective-permute-start | bytes 786440 | tf_op jit(solution)/shard_map/while/body/eval_jaxpr/ppermute | solution.py:11
  66.4 12.4 %collective-permute-start = (bf16[16,4096]{1,0:T(8,128)(2,1)S(1)}, bf16[16,4096]{1,0:T(8,128)(2,1)S(1)}, u32[]{:S(2)}, u32[]{:S(2)}) collective-permute-start(bf16[16,4096]{1,0:T(8,128)(2,1)S(1)} %copy.144), channel_id=1, source_target_pairs={{0,1},{1,2},{2,3},{3,4},{4,5},{5,6},{6,7},{7,0},{8,9},{9,10},{10,1... | collective-permute-start | bytes 393224 | tf_op jit(solution)/shard_map/while/body/eval_jaxpr/ppermute | solution.py:11
  66.5 12.2 %collective-permute-start.2 = (f32[16,32]{0,1:T(8,128)S(1)}, f32[16,32]{0,1:T(8,128)S(1)}, u32[]{:S(2)}, u32[]{:S(2)}) collective-permute-start(f32[16,32]{0,1:T(8,128)S(1)} %get-tuple-element.564), channel_id=1, source_target_pairs={{0,1},{1,2},{2,3},{3,4},{4,5},{5,6},{6,7},{7,0},{8,9},{9,10},{10,1... | collective-permute-start | bytes 6152 | tf_op jit(solution)/shard_map/while/body/eval_jaxpr/ppermute | solution.py:11
  66.5 12.3 %collective-permute-start.3 = (f32[16,32]{0,1:T(8,128)S(1)}, f32[16,32]{0,1:T(8,128)S(1)}, u32[]{:S(2)}, u32[]{:S(2)}) collective-permute-start(f32[16,32]{0,1:T(8,128)S(1)} %get-tuple-element.565), channel_id=1, source_target_pairs={{0,1},{1,2},{2,3},{3,4},{4,5},{5,6},{6,7},{7,0},{8,9},{9,10},{10,1... | collective-permute-start | bytes 6152 | tf_op jit(solution)/shard_map/while/body/eval_jaxpr/ppermute | solution.py:11
  83.2 11.7 %collective-permute-start.1 = (f32[16,4096]{1,0:T(8,128)S(1)}, f32[16,4096]{1,0:T(8,128)S(1)}, u32[]{:S(2)}, u32[]{:S(2)}) collective-permute-start(f32[16,4096]{1,0:T(8,128)S(1)} %fusion.72), channel_id=1, source_target_pairs={{0,1},{1,2},{2,3},{3,4},{4,5},{5,6},{6,7},{7,0},{8,9},{9,10},{10,1... | collective-permute-start | bytes 786440 | tf_op jit(solution)/shard_map/while/body/eval_jaxpr/ppermute | solution.py:11
  83.3 11.6 %collective-permute-start = (bf16[16,4096]{1,0:T(8,128)(2,1)S(1)}, bf16[16,4096]{1,0:T(8,128)(2,1)S(1)}, u32[]{:S(2)}, u32[]{:S(2)}) collective-permute-start(bf16[16,4096]{1,0:T(8,128)(2,1)S(1)} %copy.144), channel_id=1, source_target_pairs={{0,1},{1,2},{2,3},{3,4},{4,5},{5,6},{6,7},{7,0},{8,9},{9,10},{10,1... | collective-permute-start | bytes 393224 | tf_op jit(solution)/shard_map/while/body/eval_jaxpr/ppermute | solution.py:11
  83.4 11.4 %collective-permute-start.2 = (f32[16,32]{0,1:T(8,128)S(1)}, f32[16,32]{0,1:T(8,128)S(1)}, u32[]{:S(2)}, u32[]{:S(2)}) collective-permute-start(f32[16,32]{0,1:T(8,128)S(1)} %get-tuple-element.564), channel_id=1, source_target_pairs={{0,1},{1,2},{2,3},{3,4},{4,5},{5,6},{6,7},{7,0},{8,9},{9,10},{10,1... | collective-permute-start | bytes 6152 | tf_op jit(solution)/shard_map/while/body/eval_jaxpr/ppermute | solution.py:11
  83.4 11.5 %collective-permute-start.3 = (f32[16,32]{0,1:T(8,128)S(1)}, f32[16,32]{0,1:T(8,128)S(1)}, u32[]{:S(2)}, u32[]{:S(2)}) collective-permute-start(f32[16,32]{0,1:T(8,128)S(1)} %get-tuple-element.565), channel_id=1, source_target_pairs={{0,1},{1,2},{2,3},{3,4},{4,5},{5,6},{6,7},{7,0},{8,9},{9,10},{10,1... | collective-permute-start | bytes 6152 | tf_op jit(solution)/shard_map/while/body/eval_jaxpr/ppermute | solution.py:11
  99.3 10.9 %collective-permute-start.1 = (f32[16,4096]{1,0:T(8,128)S(1)}, f32[16,4096]{1,0:T(8,128)S(1)}, u32[]{:S(2)}, u32[]{:S(2)}) collective-permute-start(f32[16,4096]{1,0:T(8,128)S(1)} %fusion.72), channel_id=1, source_target_pairs={{0,1},{1,2},{2,3},{3,4},{4,5},{5,6},{6,7},{7,0},{8,9},{9,10},{10,1... | collective-permute-start | bytes 786440 | tf_op jit(solution)/shard_map/while/body/eval_jaxpr/ppermute | solution.py:11
  99.3 10.8 %collective-permute-start = (bf16[16,4096]{1,0:T(8,128)(2,1)S(1)}, bf16[16,4096]{1,0:T(8,128)(2,1)S(1)}, u32[]{:S(2)}, u32[]{:S(2)}) collective-permute-start(bf16[16,4096]{1,0:T(8,128)(2,1)S(1)} %copy.144), channel_id=1, source_target_pairs={{0,1},{1,2},{2,3},{3,4},{4,5},{5,6},{6,7},{7,0},{8,9},{9,10},{10,1... | collective-permute-start | bytes 393224 | tf_op jit(solution)/shard_map/while/body/eval_jaxpr/ppermute | solution.py:11
  99.5 10.7 %collective-permute-start.3 = (f32[16,32]{0,1:T(8,128)S(1)}, f32[16,32]{0,1:T(8,128)S(1)}, u32[]{:S(2)}, u32[]{:S(2)}) collective-permute-start(f32[16,32]{0,1:T(8,128)S(1)} %get-tuple-element.565), channel_id=1, source_target_pairs={{0,1},{1,2},{2,3},{3,4},{4,5},{5,6},{6,7},{7,0},{8,9},{9,10},{10,1... | collective-permute-start | bytes 6152 | tf_op jit(solution)/shard_map/while/body/eval_jaxpr/ppermute | solution.py:11
  114.5 10.9 %collective-permute-start.1 = (f32[16,4096]{1,0:T(8,128)S(1)}, f32[16,4096]{1,0:T(8,128)S(1)}, u32[]{:S(2)}, u32[]{:S(2)}) collective-permute-start(f32[16,4096]{1,0:T(8,128)S(1)} %fusion.72), channel_id=1, source_target_pairs={{0,1},{1,2},{2,3},{3,4},{4,5},{5,6},{6,7},{7,0},{8,9},{9,10},{10,1... | collective-permute-start | bytes 786440 | tf_op jit(solution)/shard_map/while/body/eval_jaxpr/ppermute | solution.py:11
  114.6 10.8 %collective-permute-start = (bf16[16,4096]{1,0:T(8,128)(2,1)S(1)}, bf16[16,4096]{1,0:T(8,128)(2,1)S(1)}, u32[]{:S(2)}, u32[]{:S(2)}) collective-permute-start(bf16[16,4096]{1,0:T(8,128)(2,1)S(1)} %copy.144), channel_id=1, source_target_pairs={{0,1},{1,2},{2,3},{3,4},{4,5},{5,6},{6,7},{7,0},{8,9},{9,10},{10,1... | collective-permute-start | bytes 393224 | tf_op jit(solution)/shard_map/while/body/eval_jaxpr/ppermute | solution.py:11
  114.7 10.7 %collective-permute-start.3 = (f32[16,32]{0,1:T(8,128)S(1)}, f32[16,32]{0,1:T(8,128)S(1)}, u32[]{:S(2)}, u32[]{:S(2)}) collective-permute-start(f32[16,32]{0,1:T(8,128)S(1)} %get-tuple-element.565), channel_id=1, source_target_pairs={{0,1},{1,2},{2,3},{3,4},{4,5},{5,6},{6,7},{7,0},{8,9},{9,10},{10,1... | collective-permute-start | bytes 6152 | tf_op jit(solution)/shard_map/while/body/eval_jaxpr/ppermute | solution.py:11
  129.8 10.9 %collective-permute-start.1 = (f32[16,4096]{1,0:T(8,128)S(1)}, f32[16,4096]{1,0:T(8,128)S(1)}, u32[]{:S(2)}, u32[]{:S(2)}) collective-permute-start(f32[16,4096]{1,0:T(8,128)S(1)} %fusion.72), channel_id=1, source_target_pairs={{0,1},{1,2},{2,3},{3,4},{4,5},{5,6},{6,7},{7,0},{8,9},{9,10},{10,1... | collective-permute-start | bytes 786440 | tf_op jit(solution)/shard_map/while/body/eval_jaxpr/ppermute | solution.py:11
  129.9 10.8 %collective-permute-start = (bf16[16,4096]{1,0:T(8,128)(2,1)S(1)}, bf16[16,4096]{1,0:T(8,128)(2,1)S(1)}, u32[]{:S(2)}, u32[]{:S(2)}) collective-permute-start(bf16[16,4096]{1,0:T(8,128)(2,1)S(1)} %copy.144), channel_id=1, source_target_pairs={{0,1},{1,2},{2,3},{3,4},{4,5},{5,6},{6,7},{7,0},{8,9},{9,10},{10,1... | collective-permute-start | bytes 393224 | tf_op jit(solution)/shard_map/while/body/eval_jaxpr/ppermute | solution.py:11
  130.0 10.7 %collective-permute-start.3 = (f32[16,32]{0,1:T(8,128)S(1)}, f32[16,32]{0,1:T(8,128)S(1)}, u32[]{:S(2)}, u32[]{:S(2)}) collective-permute-start(f32[16,32]{0,1:T(8,128)S(1)} %get-tuple-element.565), channel_id=1, source_target_pairs={{0,1},{1,2},{2,3},{3,4},{4,5},{5,6},{6,7},{7,0},{8,9},{9,10},{10,1... | collective-permute-start | bytes 6152 | tf_op jit(solution)/shard_map/while/body/eval_jaxpr/ppermute | solution.py:11
  (15 other events, 209.6 us)
where the time goes:
time: 165 us
  waiting for transfers between devices  83.6 us (51%)
  starting transfers between devices  27.9 us (17%)
  local copies, waits for them, and re-layouts  16 us (10%)
  other arithmetic  14 us (8%)
  blocking collectives  8.17 us (5%)
  matrix products  6.6 us (4%)
  loops' own time  5.46 us (3%)
  between operations  2.83 us (2%)
    ppermute x30, waiting for transfers between devices, shifted(): lax.ppermute(value, axis, [(i, (i + by) % length) for i in range(length)])  76.3 us
    ppermute x30, starting transfers between devices, shifted(): lax.ppermute(value, axis, [(i, (i + by) % length) for i in range(length)])  16.9 us
    all_to_all x1, blocking collectives, local(): lax.all_to_all(blended[None], 'grp', split_axis=1, concat_axis=0, tiled=T...  8.17 us
    another operation x1, loops' own time, local(): lax.fori_loop(0, members - 1, cycle_turn, (local_q, start))  5.46 us
    dynamic_slice x8, local copies, waits for them, and re-layouts, visit_block(): query_pos = block_order[source] * row_count + query_lane  5.17 us
    lt x8, other arithmetic, allowed_for(): cache_ok = block_index * cached + cache_lane < hit_limit  4.57 us
    all_to_all x1, starting transfers between devices, local(): lax.all_to_all(new_keys, 'grp', split_axis=0, concat_axis=1, tiled=True)  4.26 us
    all_to_all x1, waiting for transfers between devices, local(): lax.all_to_all(queries, 'grp', split_axis=0, concat_axis=1, tiled=True)  3.68 us
  transfers between devices with their start and end apart: 33, of which 17 were waited for; matrix products, arithmetic and copies ran while one was open for 2% of the time, Pallas kernels for 0%

commit v1 on v0

v1 whole, which is shorter than its diff:
```python
import functools
import math

import jax
import jax.numpy as jnp
from jax import lax
from jax.experimental import pallas as pl
from jax.experimental.pallas import tpu as pltpu
from jax.sharding import PartitionSpec as P

HEAD_DIM = 128
FLOOR = -1e30
MESH = pl.DeviceIdType.MESH


def kernel(
    n_blk, n_grp, size, per_chunk,
    hits_ref, counts_ref, assign_ref, q_ref, nk_ref, nv_ref, ck_ref, cv_ref, out_ref,
    k_own, v_own, k_buf, v_buf, vt_buf, fresh_own, fresh_buf, q_buf, o_buf, r_buf,
    load_sem, kv_send, kv_recv, fresh_send, fresh_recv, q_send, q_recv, o_send, o_recv,
):
    blk, grp = lax.axis_index("blk"), lax.axis_index("grp")
    n_dev = n_blk * n_grp
    cluster, member = blk // size, blk % size
    n_cluster = n_blk // size
    requests, rows, heads, dim = q_ref.shape
    group = heads // size
    half = fresh_own.shape[2] // 2
    cached = k_own.shape[0]
    block_rows = rows * n_grp
    n_chunk = n_blk // per_chunk
    lanes = per_chunk * block_rows * group
    rate = dim ** -0.5 * math.log2(math.e)

    load_k = pltpu.make_async_copy(ck_ref.at[0], k_own, load_sem.at[0])
    load_v = pltpu.make_async_copy(cv_ref.at[0], v_own, load_sem.at[1])
    load_k.start()
    load_v.start()

    barrier = pltpu.get_barrier_semaphore()

    def peer(step):
        return lax.rem(blk + step // n_grp, n_blk), lax.rem(grp + step % n_grp, n_grp)

    def greet(step, carry):
        to_blk, to_grp = peer(step)
        pl.semaphore_signal(
            barrier, inc=1, device_id={"blk": to_blk, "grp": to_grp}, device_id_type=MESH
        )
        return carry

    lax.fori_loop(1, n_dev, greet, 0)

    fresh_own[...] = jnp.zeros_like(fresh_own)
    for r in range(requests):
        for h in range(size):
            cols = slice(h * dim, (h + 1) * dim)
            fresh_own[r, h, 0:rows, :] = nk_ref[r, :, cols].astype(jnp.float32)
            fresh_own[r, h, half : half + rows, :] = nv_ref[r, :, cols].astype(jnp.float32)

    pl.semaphore_wait(barrier, n_dev - 1)

    def q_piece(to_grp, head):
        return q_ref.at[to_grp, :, pl.ds(pl.multiple_of(head * group, group), group), :]

    def send_q(step, carry):
        to_blk, to_grp = peer(step)
        pltpu.make_async_remote_copy(
            src_ref=q_piece(to_grp, to_blk % size),
            dst_ref=q_buf.at[blk, grp],
            send_sem=q_send,
            recv_sem=q_recv.at[blk // per_chunk],
            device_id={"blk": to_blk, "grp": to_grp},
            device_id_type=MESH,
        ).start()
        return carry

    lax.fori_loop(1, n_dev, send_q, 0)
    pltpu.make_async_copy(
        q_piece(grp, member), q_buf.at[blk, grp], q_recv.at[blk // per_chunk]
    ).start()

    load_k.wait()
    load_v.wait()
    kv_copies = []
    for step in range(1, size):
        to_member = lax.rem(member + step, size)
        cols = pl.ds(pl.multiple_of(to_member * dim, dim), dim)
        for which, (own, buf) in enumerate(((k_own, k_buf), (v_own, v_buf))):
            copy = pltpu.make_async_remote_copy(
                src_ref=own.at[:, cols],
                dst_ref=buf.at[member],
                send_sem=kv_send.at[step, which],
                recv_sem=kv_recv.at[step, which],
                device_id={"blk": cluster * size + to_member, "grp": grp},
                device_id_type=MESH,
            )
            copy.start()
            kv_copies.append(copy)
    own_cols = pl.ds(pl.multiple_of(member * dim, dim), dim)
    for which, (own, buf) in enumerate(((k_own, k_buf), (v_own, v_buf))):
        copy = pltpu.make_async_copy(own.at[:, own_cols], buf.at[member], kv_recv.at[0, which])
        copy.start()
        kv_copies.append(copy)

    def send_fresh(step, carry):
        to_member = lax.rem(member + step // n_grp, size)
        to_grp = lax.rem(grp + step % n_grp, n_grp)
        pltpu.make_async_remote_copy(
            src_ref=fresh_own.at[to_grp, to_member],
            dst_ref=fresh_buf.at[member * n_grp + grp],
            send_sem=fresh_send,
            recv_sem=fresh_recv,
            device_id={"blk": cluster * size + to_member, "grp": to_grp},
            device_id_type=MESH,
        ).start()
        return carry

    lax.fori_loop(1, size * n_grp, send_fresh, 0)
    pltpu.make_async_copy(
        fresh_own.at[grp, member], fresh_buf.at[member * n_grp + grp], fresh_recv
    ).start()

    pltpu.make_async_copy(fresh_buf, fresh_buf, fresh_recv).wait()
    for copy in kv_copies:
        copy.wait()

    hit = hits_ref[0]
    count = counts_ref[0]
    n_fresh = size * n_grp * 2 * half
    fresh = fresh_buf[...].reshape(n_fresh, dim).astype(jnp.bfloat16)
    for s in range(size):
        vt_buf[:, s * cached : (s + 1) * cached] = v_buf[s].T
    vt_buf[:, size * cached :] = fresh.T

    key_row = lax.broadcasted_iota(jnp.int32, (n_fresh, 1), 0)
    key_from = key_row // (2 * half)
    key_pos = (key_from % n_grp) * rows + key_row % (2 * half)
    for s in range(size):
        base = assign_ref[0, cluster * size + s] * block_rows
        key_pos = key_pos + jnp.where(key_from // n_grp == s, base, 0)
    key_real = key_row % (2 * half) < rows
    key_pos = jnp.where(key_real, key_pos, n_blk * block_rows)
    first = cluster * size * cached
    cached_ok = first + lax.broadcasted_iota(jnp.int32, (size * cached, 1), 0) < hit

    def chunk_step(turn, carry):
        chunk = lax.rem(blk // per_chunk + turn + 1, n_chunk)
        blocks = pl.ds(chunk * per_chunk, per_chunk)
        pltpu.make_async_copy(q_buf.at[blocks], q_buf.at[blocks], q_recv.at[chunk]).wait()
        queries = q_buf[blocks].reshape(lanes, dim)
        lane = lax.broadcasted_iota(jnp.int32, (1, lanes), 1)
        pos = (lane // group) % block_rows
        for j in range(per_chunk):
            base = assign_ref[0, chunk * per_chunk + j] * block_rows
            pos = pos + jnp.where(lane // (group * block_rows) == j, base, 0)
        nt = (((1,), (1,)), ((), ()))
        keys = k_buf[...].reshape(size * cached, dim)
        s_old = lax.dot_general(keys, queries, nt, preferred_element_type=jnp.float32)
        s_new = lax.dot_general(fresh, queries, nt, preferred_element_type=jnp.float32)
        s_old = jnp.where(cached_ok, s_old, FLOOR)
        s_new = jnp.where(key_pos <= pos, s_new, FLOOR)
        top = jnp.maximum(
            jnp.max(s_old, axis=0, keepdims=True), jnp.max(s_new, axis=0, keepdims=True)
        )
        top = jnp.maximum(top, 0.1 * FLOOR)
        p_old = jnp.exp2((s_old - top) * rate)
        p_new = jnp.exp2((s_new - top) * rate)
        weight = jnp.sum(p_old, axis=0, keepdims=True) + jnp.sum(p_new, axis=0, keepdims=True)
        p_new = pltpu.roll(p_new, half, 0)
        nn = (((1,), (0,)), ((), ()))
        mixed = lax.dot_general(
            vt_buf[:, : size * cached], p_old.astype(jnp.bfloat16), nn,
            preferred_element_type=jnp.float32,
        ) + lax.dot_general(
            vt_buf[:, size * cached :], p_new.astype(jnp.bfloat16), nn,
            preferred_element_type=jnp.float32,
        )
        mixed = jnp.where(pos < count, mixed / jnp.maximum(weight, 1.0), 0.0)
        level = top * rate + jnp.log2(jnp.maximum(weight, 1e-30))
        n_dest = per_chunk * n_grp
        values = mixed.T.reshape(per_chunk, n_grp, rows, group, dim)
        levels = jnp.broadcast_to(level, (dim, lanes)).T.reshape(n_dest, rows, group, dim)
        spot = lax.broadcasted_iota(jnp.int32, (1, 1, dim), 2)
        tile = jnp.zeros((n_dest, group, dim), jnp.float32)
        for i in range(rows):
            tile = jnp.where(spot % rows == i, levels[:, i], tile)
        high = tile.astype(jnp.bfloat16).astype(jnp.float32)
        middle = (tile - high).astype(jnp.bfloat16).astype(jnp.float32)
        low = tile - high - middle
        tile = jnp.where(spot < rows, high, jnp.where(spot < 2 * rows, middle, low))
        tile = jnp.where(spot < 3 * rows, tile, 0.0)
        o_buf[blocks, :, 0:rows] = values.astype(jnp.bfloat16)
        o_buf[blocks, :, rows : rows + 1] = tile.astype(jnp.bfloat16).reshape(
            per_chunk, n_grp, 1, group, dim
        )

        def send_out(index, carry):
            to_blk = chunk * per_chunk + index // n_grp
            to_grp = index % n_grp
            mine = jnp.logical_and(to_blk == blk, to_grp == grp)

            @pl.when(mine)
            def _():
                pltpu.make_async_copy(o_buf.at[blk, grp], r_buf.at[blk, grp], o_recv).start()

            @pl.when(jnp.logical_not(mine))
            def _():
                pltpu.make_async_remote_copy(
                    src_ref=o_buf.at[to_blk, to_grp],
                    dst_ref=r_buf.at[blk, grp],
                    send_sem=o_send,
                    recv_sem=o_recv,
                    device_id={"blk": to_blk, "grp": to_grp},
                    device_id_type=MESH,
                ).start()

            return carry

        lax.fori_loop(0, n_dest, send_out, 0)
        return carry

    lax.fori_loop(0, n_chunk, chunk_step, 0)

    pltpu.make_async_copy(r_buf, r_buf, o_recv).wait()

    def parts(c, h, r):
        tile = r_buf[c * size + h, r, rows].astype(jnp.float32)
        return tile + pltpu.roll(tile, dim - rows, 1) + pltpu.roll(tile, dim - 2 * rows, 1)

    def finish(r, carry):
        for h in range(size):
            levels = [parts(c, h, r) for c in range(n_cluster)]
            top = functools.reduce(jnp.maximum, levels)
            scales = [jnp.exp2(level - top) for level in levels]
            total = functools.reduce(jnp.add, scales)
            scales = [scale / total for scale in scales]
            for i in range(rows):
                terms = [
                    scales[c][:, i : i + 1] * r_buf[c * size + h, r, i].astype(jnp.float32)
                    for c in range(n_cluster)
                ]
                out_ref[r, i, h * group : (h + 1) * group, :] = functools.reduce(
                    jnp.add, terms
                ).astype(out_ref.dtype)
        return carry

    lax.fori_loop(0, requests, finish, 0)

    rest = n_dev - 1
    q_flat = q_buf.at[0 : n_blk - 1]
    pltpu.make_async_copy(q_flat, q_flat, q_send).wait()
    q_flat = q_buf.at[0, 0 : n_grp - 1]
    pltpu.make_async_copy(q_flat, q_flat, q_send).wait()
    r_flat = r_buf.at[0 : n_blk - 1]
    pltpu.make_async_copy(r_flat, r_flat, o_send).wait()
    r_flat = r_buf.at[0, 0 : n_grp - 1]
    pltpu.make_async_copy(r_flat, r_flat, o_send).wait()
    f_flat = fresh_buf.at[0 : size * n_grp - 1]
    pltpu.make_async_copy(f_flat, f_flat, fresh_send).wait()


def solution(mesh):
    n_blk, n_grp = mesh.shape["blk"], mesh.shape["grp"]

    def local(queries, cache_keys, cache_values, new_keys, new_values, hits, counts, assign):
        requests, rows, width = queries.shape
        cached, kv_width = cache_keys.shape[1:]
        size = kv_width // HEAD_DIM
        heads = width // HEAD_DIM
        group = heads // size
        half = max(rows, 4)
        per_chunk = 2
        bf, f32 = jnp.bfloat16, jnp.float32
        vmem = pl.BlockSpec(memory_space=pltpu.VMEM)
        smem = pl.BlockSpec(memory_space=pltpu.SMEM)
        hbm = pl.BlockSpec(memory_space=pl.ANY)
        n_keys = size * cached + size * n_grp * 2 * half
        out = pl.pallas_call(
            functools.partial(kernel, n_blk, n_grp, size, per_chunk),
            out_shape=jax.ShapeDtypeStruct((requests, rows, heads, HEAD_DIM), bf),
            in_specs=[smem, smem, smem, vmem, vmem, vmem, hbm, hbm],
            out_specs=vmem,
            scratch_shapes=[
                pltpu.VMEM((cached, kv_width), bf),
                pltpu.VMEM((cached, kv_width), bf),
                pltpu.VMEM((size, cached, HEAD_DIM), bf),
                pltpu.VMEM((size, cached, HEAD_DIM), bf),
                pltpu.VMEM((HEAD_DIM, n_keys), bf),
                pltpu.VMEM((requests, size, 2 * half, HEAD_DIM), f32),
                pltpu.VMEM((size * n_grp, 2 * half, HEAD_DIM), f32),
                pltpu.VMEM((n_blk, n_grp, rows, group, HEAD_DIM), bf),
                pltpu.VMEM((n_blk, n_grp, rows + 1, group, HEAD_DIM), bf),
                pltpu.VMEM((n_blk, n_grp, rows + 1, group, HEAD_DIM), bf),
                pltpu.SemaphoreType.DMA((2,)),
                pltpu.SemaphoreType.DMA((size, 2)),
                pltpu.SemaphoreType.DMA((size, 2)),
                pltpu.SemaphoreType.DMA,
                pltpu.SemaphoreType.DMA,
                pltpu.SemaphoreType.DMA,
                pltpu.SemaphoreType.DMA((n_blk // per_chunk,)),
                pltpu.SemaphoreType.DMA,
                pltpu.SemaphoreType.DMA,
            ],
            compiler_params=pltpu.CompilerParams(
                collective_id=0, has_side_effects=True, vmem_limit_bytes=60 * 2**20
            ),
        )(
            hits, counts, assign,
            queries.reshape(requests, rows, heads, HEAD_DIM),
            new_keys, new_values, cache_keys, cache_values,
        )
        return out.reshape(requests, rows, width)

    return jax.shard_map(
        local,
        mesh=mesh,
        in_specs=(
            P(None, ("blk", "grp"), None),
            P("grp", "blk", None),
            P("grp", "blk", None),
            P(None, ("blk", "grp"), None),
            P(None, ("blk", "grp"), None),
            P("grp"),
            P("grp"),
            P("grp", None),
        ),
        out_specs=P(None, ("blk", "grp"), None),
        check_vma=False,
    )
```

time: 165 us -> 42.1 us (0.26)
  waiting for transfers between devices: 83.6 us -> 0 us
  Pallas kernels: 0 us -> 37.2 us
  starting transfers between devices: 27.9 us -> 0 us
  other arithmetic: 14 us -> 0 us
  local copies, waits for them, and re-layouts: 16 us -> 3.31 us
  blocking collectives: 8.17 us -> 0 us
  matrix products: 6.6 us -> 0 us
  loops' own time: 5.46 us -> 0 us
    ppermute x30 -> x0, waiting for transfers between devices: 76.3 us -> none  [shifted(): lax.ppermute(value, axis, [(i, (i + by) % length) for i in range(length)])]
    pallas_call x0 -> x1, Pallas kernels: none -> 37.2 us  [local(): pl.pallas_call(functools.partial(kernel, n_blk, n_grp, size, per_chunk),...]
    ppermute x30 -> x0, starting transfers between devices: 16.9 us -> none  [shifted(): lax.ppermute(value, axis, [(i, (i + by) % length) for i in range(length)])]
    all_to_all x3 -> x0, starting transfers between devices: 11 us -> none  [the longest x1 4.26 us: local(): lax.all_to_all(new_keys, 'grp', split_axis=0, concat_axis=1, tiled=True)]
    all_to_all x1 -> x0, blocking collectives: 8.17 us -> none  [local(): lax.all_to_all(blended[None], 'grp', split_axis=1, concat_axis=0, tiled=T...]
    all_to_all x3 -> x0, waiting for transfers between devices: 7.35 us -> none  [the longest x1 3.68 us: local(): lax.all_to_all(queries, 'grp', split_axis=0, concat_axis=1, tiled=True)]
    dot_general x16 -> x0, matrix products: 6.6 us -> none  [the longest x8 3.53 us: partial_block(): jnp.einsum('qkgd,nkd->kgqn', query_heads, key_heads, preferred_element_ty...]
    another operation x1 -> x0, loops' own time: 5.46 us -> none  [local(): lax.fori_loop(0, members - 1, cycle_turn, (local_q, start))]
  transfers between devices with their start and end apart: 33 -> 0, of which waited for: 17 -> 0; matrix products, arithmetic and copies ran while one was open for 2% -> 0% of each run, Pallas kernels for 0% -> 0%
where the time goes in v1:
time: 42.1 us; the launch traced here: 41.9 us
  Pallas kernels  37.2 us (88%)
  local copies, waits for them, and re-layouts  3.31 us (8%)
  between operations  1.31 us (3%)
    pallas_call x1, Pallas kernels, local(): pl.pallas_call(functools.partial(kernel, n_blk, n_grp, size, per_chunk),...  37.2 us
    reshape x1, local copies, waits for them, and re-layouts, local(): queries.reshape(requests, rows, heads, HEAD_DIM)  1.71 us
    reshape x1, local copies, waits for them, and re-layouts, local(): return out.reshape(requests, rows, width)  1.59 us

profile of v1, /device:TPU:0, one launch (start us, length us, event | category | flops | bytes accessed | tf_op | source)
XLA Modules:
  0.0 41.9 jit_solution(11699424969357951712)
XLA Ops:
  1.3 1.7 %reshape.6.q_ref = bf16[4,4,32,128]{3,2,1,0:T(8,128)(2,1)} reshape(bf16[4,4,4096]{2,1,0:T(4,128)(2,1)} %param.8) | data formatting | bytes 262144 | tf_op jit(solution)/shard_map/reshape | solution.py:310
  3.0 37.2 %shard_map.82 = bf16[4,4,32,128]{3,2,1,0:T(8,128)(2,1)} custom-call(s32[1]{0:T(128)S(6)} %copy.9.hits_ref, s32[1]{0:T(128)S(6)} %copy.10.counts_ref, s32[1,8]{1,0:T(1,128)} %assign_ref.1, bf16[4,4,32,128]{3,2,1,0:T(8,128)(2,1)} %reshape.6.q_ref, bf16[4,4,512]{2,1,0:T(4,128)(2,1)} %nk_ref.1, bf16[4,4,512]{2,1,0:T(4,128)(2,1)} %nv_ref.1, ...), custom_call_target="tpu_custom_call" | custom-call | tf_op jit(solution)/shard_map/pallas_call | solution.py:279
  40.3 1.6 %reshape.7 = bf16[4,4,4096]{2,1,0:T(4,128)(2,1)} reshape(bf16[4,4,32,128]{3,2,1,0:T(8,128)(2,1)} %shard_map.82) | data formatting | bytes 262144 | tf_op jit(solution)/shard_map/reshape | solution.py:313

commit v2 on v1

--- a/solution.py
+++ b/solution.py
@@ -16,14 +16,14 @@
 def kernel(
     n_blk, n_grp, size, per_chunk,
     hits_ref, counts_ref, assign_ref, q_ref, nk_ref, nv_ref, ck_ref, cv_ref, out_ref,
-    k_own, v_own, k_buf, v_buf, vt_buf, fresh_own, fresh_buf, q_buf, o_buf, r_buf,
-    load_sem, kv_send, kv_recv, fresh_send, fresh_recv, q_send, q_recv, o_send, o_recv,
+    q_own, k_own, v_own, k_buf, v_buf, vt_buf, fresh_own, fresh_buf, q_buf, o_buf, r_buf,
+    known_sem, load_sem, kv_send, kv_recv, fresh_send, fresh_recv, q_send, q_recv, o_send, o_recv,
 ):
     blk, grp = lax.axis_index("blk"), lax.axis_index("grp")
     n_dev = n_blk * n_grp
     cluster, member = blk // size, blk % size
     n_cluster = n_blk // size
-    requests, rows, heads, dim = q_ref.shape
+    requests, rows, heads, dim = q_own.shape
     group = heads // size
     half = fresh_own.shape[2] // 2
     cached = k_own.shape[0]
@@ -42,43 +42,32 @@
     def peer(step):
         return lax.rem(blk + step // n_grp, n_blk), lax.rem(grp + step % n_grp, n_grp)
 
-    def greet(step, carry):
-        to_blk, to_grp = peer(step)
-        pl.semaphore_signal(
-            barrier, inc=1, device_id={"blk": to_blk, "grp": to_grp}, device_id_type=MESH
-        )
-        return carry
-
-    lax.fori_loop(1, n_dev, greet, 0)
-
-    fresh_own[...] = jnp.zeros_like(fresh_own)
+    grp_peers = [(blk, lax.rem(grp + step, n_grp)) for step in range(1, n_grp)]
+    cluster_peers = [
+        (cluster * size + lax.rem(member + step, size), grp) for step in range(1, size)
+    ]
+    far_peers = [(lax.rem(blk + step * size, n_blk), grp) for step in range(1, n_cluster)]
+
+    def meet(sem, peers):
+        for to_blk, to_grp in peers:
+            pl.semaphore_signal(
+                sem, inc=1, device_id={"blk": to_blk, "grp": to_grp}, device_id_type=MESH
+            )
+
+    near = grp_peers + cluster_peers + far_peers
+    meet(barrier, near)
+
+    gap = jnp.zeros((half - rows, dim), jnp.float32)
     for r in range(requests):
         for h in range(size):
             cols = slice(h * dim, (h + 1) * dim)
-            fresh_own[r, h, 0:rows, :] = nk_ref[r, :, cols].astype(jnp.float32)
-            fresh_own[r, h, half : half + rows, :] = nv_ref[r, :, cols].astype(jnp.float32)
-
-    pl.semaphore_wait(barrier, n_dev - 1)
-
-    def q_piece(to_grp, head):
-        return q_ref.at[to_grp, :, pl.ds(pl.multiple_of(head * group, group), group), :]
-
-    def send_q(step, carry):
-        to_blk, to_grp = peer(step)
-        pltpu.make_async_remote_copy(
-            src_ref=q_piece(to_grp, to_blk % size),
-            dst_ref=q_buf.at[blk, grp],
-            send_sem=q_send,
-            recv_sem=q_recv.at[blk // per_chunk],
-            device_id={"blk": to_blk, "grp": to_grp},
-            device_id_type=MESH,
-        ).start()
-        return carry
-
-    lax.fori_loop(1, n_dev, send_q, 0)
-    pltpu.make_async_copy(
-        q_piece(grp, member), q_buf.at[blk, grp], q_recv.at[blk // per_chunk]
-    ).start()
+            pieces = [nk_ref[r, :, cols].astype(jnp.float32), nv_ref[r, :, cols].astype(jnp.float32)]
+            if half > rows:
+                pieces = [pieces[0], gap, pieces[1], gap]
+            fresh_own[r, h] = jnp.concatenate(pieces, 0).astype(jnp.bfloat16)
+        q_own[r] = q_ref[r].reshape(rows, heads, dim)
+
+    pl.semaphore_wait(barrier, len(near))
 
     load_k.wait()
     load_v.wait()
@@ -103,6 +92,11 @@
         copy.start()
         kv_copies.append(copy)
 
+    meet(known_sem.at[0], grp_peers)
+    pl.semaphore_wait(known_sem.at[0], len(grp_peers))
+    meet(known_sem.at[1], cluster_peers)
+    pl.semaphore_wait(known_sem.at[1], len(cluster_peers))
+
     def send_fresh(step, carry):
         to_member = lax.rem(member + step // n_grp, size)
         to_grp = lax.rem(grp + step % n_grp, n_grp)
@@ -121,6 +115,26 @@
         fresh_own.at[grp, member], fresh_buf.at[member * n_grp + grp], fresh_recv
     ).start()
 
+    def q_piece(to_grp, head):
+        return q_own.at[to_grp, :, pl.ds(pl.multiple_of(head * group, group), group), :]
+
+    def send_q(step, carry):
+        to_blk, to_grp = peer(step)
+        pltpu.make_async_remote_copy(
+            src_ref=q_piece(to_grp, to_blk % size),
+            dst_ref=q_buf.at[blk, grp],
+            send_sem=q_send,
+            recv_sem=q_recv.at[blk // per_chunk],
+            device_id={"blk": to_blk, "grp": to_grp},
+            device_id_type=MESH,
+        ).start()
+        return carry
+
+    lax.fori_loop(1, n_dev, send_q, 0)
+    pltpu.make_async_copy(
+        q_piece(grp, member), q_buf.at[blk, grp], q_recv.at[blk // per_chunk]
+    ).start()
+
     pltpu.make_async_copy(fresh_buf, fresh_buf, fresh_recv).wait()
     for copy in kv_copies:
         copy.wait()
@@ -128,7 +142,7 @@
     hit = hits_ref[0]
     count = counts_ref[0]
     n_fresh = size * n_grp * 2 * half
-    fresh = fresh_buf[...].reshape(n_fresh, dim).astype(jnp.bfloat16)
+    fresh = fresh_buf[...].reshape(n_fresh, dim)
     for s in range(size):
         vt_buf[:, s * cached : (s + 1) * cached] = v_buf[s].T
     vt_buf[:, size * cached :] = fresh.T
@@ -282,16 +296,18 @@
             in_specs=[smem, smem, smem, vmem, vmem, vmem, hbm, hbm],
             out_specs=vmem,
             scratch_shapes=[
+                pltpu.VMEM((requests, rows, heads, HEAD_DIM), bf),
                 pltpu.VMEM((cached, kv_width), bf),
                 pltpu.VMEM((cached, kv_width), bf),
                 pltpu.VMEM((size, cached, HEAD_DIM), bf),
                 pltpu.VMEM((size, cached, HEAD_DIM), bf),
                 pltpu.VMEM((HEAD_DIM, n_keys), bf),
-                pltpu.VMEM((requests, size, 2 * half, HEAD_DIM), f32),
-                pltpu.VMEM((size * n_grp, 2 * half, HEAD_DIM), f32),
+                pltpu.VMEM((requests, size, 2 * half, HEAD_DIM), bf),
+                pltpu.VMEM((size * n_grp, 2 * half, HEAD_DIM), bf),
                 pltpu.VMEM((n_blk, n_grp, rows, group, HEAD_DIM), bf),
                 pltpu.VMEM((n_blk, n_grp, rows + 1, group, HEAD_DIM), bf),
                 pltpu.VMEM((n_blk, n_grp, rows + 1, group, HEAD_DIM), bf),
+                pltpu.SemaphoreType.REGULAR((2,)),
                 pltpu.SemaphoreType.DMA((2,)),
                 pltpu.SemaphoreType.DMA((size, 2)),
                 pltpu.SemaphoreType.DMA((size, 2)),
@@ -307,8 +323,7 @@
             ),
         )(
             hits, counts, assign,
-            queries.reshape(requests, rows, heads, HEAD_DIM),
-            new_keys, new_values, cache_keys, cache_values,
+            queries, new_keys, new_values, cache_keys, cache_values,
         )
         return out.reshape(requests, rows, width)
 

time: 42.1 us -> 37 us (0.88)
  Pallas kernels: 37.2 us -> 33.9 us
  local copies, waits for them, and re-layouts: 3.31 us -> 1.59 us
    pallas_call x1, Pallas kernels: 37.2 us -> 33.9 us  [local(): pl.pallas_call(functools.partial(kernel, n_blk, n_grp, size, per_chunk),...]
    reshape x1 -> x0, local copies, waits for them, and re-layouts: 1.71 us -> none  [local(): queries.reshape(requests, rows, heads, HEAD_DIM)]
where the time goes in v2:
time: 37 us; the launch traced here: 36.8 us
  Pallas kernels  33.9 us (92%)
  local copies, waits for them, and re-layouts  1.59 us (4%)
  between operations  1.3 us (4%)
    pallas_call x1, Pallas kernels, local(): pl.pallas_call(functools.partial(kernel, n_blk, n_grp, size, per_chunk),...  33.9 us
    reshape x1, local copies, waits for them, and re-layouts, local(): return out.reshape(requests, rows, width)  1.59 us

profile of v2, /device:TPU:0, one launch (start us, length us, event | category | flops | bytes accessed | tf_op | source)
XLA Modules:
  0.0 36.8 jit_solution(17174881833585604723)
XLA Ops:
  1.3 33.9 %shard_map.82 = bf16[4,4,32,128]{3,2,1,0:T(8,128)(2,1)} custom-call(s32[1]{0:T(128)S(6)} %copy.9.hits_ref, s32[1]{0:T(128)S(6)} %copy.10.counts_ref, s32[1,8]{1,0:T(1,128)} %assign_ref.1, bf16[4,4,4096]{2,1,0:T(4,128)(2,1)} %q_ref.1, bf16[4,4,512]{2,1,0:T(4,128)(2,1)} %nk_ref.1, bf16[4,4,512]{2,1,0:T(4,128)(2,1)} %nv_ref.1, bf16[1,448,512]{2,1,0:T(8,128)(2,1)} %ck_ref.1, ...), custom_call_target="tpu_custom_call" | custom-call | tf_op jit(solution)/shard_map/pallas_call | solution.py:293
  35.2 1.6 %reshape.3 = bf16[4,4,4096]{2,1,0:T(4,128)(2,1)} reshape(bf16[4,4,32,128]{3,2,1,0:T(8,128)(2,1)} %shard_map.82) | data formatting | bytes 262144 | tf_op jit(solution)/shard_map/reshape | solution.py:328

commit v3 on v2

--- a/solution.py
+++ b/solution.py
@@ -15,9 +15,9 @@
 
 def kernel(
     n_blk, n_grp, size, per_chunk,
-    hits_ref, counts_ref, assign_ref, q_ref, nk_ref, nv_ref, ck_ref, cv_ref, out_ref,
-    q_own, k_own, v_own, k_buf, v_buf, vt_buf, fresh_own, fresh_buf, q_buf, o_buf, r_buf,
-    known_sem, load_sem, kv_send, kv_recv, fresh_send, fresh_recv, q_send, q_recv, o_send, o_recv,
+    hits_ref, counts_ref, assign_ref, q_hbm, nk_hbm, nv_hbm, ck_ref, cv_ref, out_ref,
+    q_ref, nk_ref, nv_ref, q_own, k_own, v_own, k_buf, v_buf, vt_buf, fresh_own, fresh_buf, q_buf, o_buf, r_buf, p_buf, w_buf, l_own, l_buf, scale_buf,
+    known_sem, load_sem, kv_send, kv_recv, fresh_send, fresh_recv, q_send, q_recv, o_send, o_recv, l_send, l_recv,
 ):
     blk, grp = lax.axis_index("blk"), lax.axis_index("grp")
     n_dev = n_blk * n_grp
@@ -29,13 +29,9 @@
     cached = k_own.shape[0]
     block_rows = rows * n_grp
     n_chunk = n_blk // per_chunk
-    lanes = per_chunk * block_rows * group
+    span = block_rows * group
+    lanes = per_chunk * span
     rate = dim ** -0.5 * math.log2(math.e)
-
-    load_k = pltpu.make_async_copy(ck_ref.at[0], k_own, load_sem.at[0])
-    load_v = pltpu.make_async_copy(cv_ref.at[0], v_own, load_sem.at[1])
-    load_k.start()
-    load_v.start()
 
     barrier = pltpu.get_barrier_semaphore()
 
@@ -56,6 +52,21 @@
 
     near = grp_peers + cluster_peers + far_peers
     meet(barrier, near)
+
+    load_k = pltpu.make_async_copy(ck_ref.at[0], k_own, load_sem.at[0])
+    load_v = pltpu.make_async_copy(cv_ref.at[0], v_own, load_sem.at[1])
+    small = [
+        pltpu.make_async_copy(source, target, load_sem.at[2 + i])
+        for i, (source, target) in enumerate(
+            ((q_hbm, q_ref), (nk_hbm, nk_ref), (nv_hbm, nv_ref))
+        )
+    ]
+    load_k.start()
+    load_v.start()
+    for copy in small:
+        copy.start()
+    for copy in small:
+        copy.wait()
 
     gap = jnp.zeros((half - rows, dim), jnp.float32)
     for r in range(requests):
@@ -69,28 +80,32 @@
 
     pl.semaphore_wait(barrier, len(near))
 
+    own_cols = pl.ds(pl.multiple_of(member * dim, dim), dim)
+
+    def send_heads(which, own, buf):
+        copies = []
+        for step in range(1, size):
+            to_member = lax.rem(member + step, size)
+            cols = pl.ds(pl.multiple_of(to_member * dim, dim), dim)
+            copies.append(
+                pltpu.make_async_remote_copy(
+                    src_ref=own.at[:, cols],
+                    dst_ref=buf.at[member],
+                    send_sem=kv_send.at[step, which],
+                    recv_sem=kv_recv.at[step, which],
+                    device_id={"blk": cluster * size + to_member, "grp": grp},
+                    device_id_type=MESH,
+                )
+            )
+        copies.append(
+            pltpu.make_async_copy(own.at[:, own_cols], buf.at[member], kv_recv.at[0, which])
+        )
+        for copy in copies:
+            copy.start()
+        return copies
+
     load_k.wait()
-    load_v.wait()
-    kv_copies = []
-    for step in range(1, size):
-        to_member = lax.rem(member + step, size)
-        cols = pl.ds(pl.multiple_of(to_member * dim, dim), dim)
-        for which, (own, buf) in enumerate(((k_own, k_buf), (v_own, v_buf))):
-            copy = pltpu.make_async_remote_copy(
-                src_ref=own.at[:, cols],
-                dst_ref=buf.at[member],
-                send_sem=kv_send.at[step, which],
-                recv_sem=kv_recv.at[step, which],
-                device_id={"blk": cluster * size + to_member, "grp": grp},
-                device_id_type=MESH,
-            )
-            copy.start()
-            kv_copies.append(copy)
-    own_cols = pl.ds(pl.multiple_of(member * dim, dim), dim)
-    for which, (own, buf) in enumerate(((k_own, k_buf), (v_own, v_buf))):
-        copy = pltpu.make_async_copy(own.at[:, own_cols], buf.at[member], kv_recv.at[0, which])
-        copy.start()
-        kv_copies.append(copy)
+    k_copies = send_heads(0, k_own, k_buf)
 
     meet(known_sem.at[0], grp_peers)
     pl.semaphore_wait(known_sem.at[0], len(grp_peers))
@@ -119,7 +134,7 @@
         return q_own.at[to_grp, :, pl.ds(pl.multiple_of(head * group, group), group), :]
 
     def send_q(step, carry):
-        to_blk, to_grp = peer(step)
+        to_blk, to_grp = peer(n_dev - step)
         pltpu.make_async_remote_copy(
             src_ref=q_piece(to_grp, to_blk % size),
             dst_ref=q_buf.at[blk, grp],
@@ -135,16 +150,17 @@
         q_piece(grp, member), q_buf.at[blk, grp], q_recv.at[blk // per_chunk]
     ).start()
 
+    load_v.wait()
+    v_copies = send_heads(1, v_own, v_buf)
+
     pltpu.make_async_copy(fresh_buf, fresh_buf, fresh_recv).wait()
-    for copy in kv_copies:
+    for copy in k_copies:
         copy.wait()
 
     hit = hits_ref[0]
     count = counts_ref[0]
     n_fresh = size * n_grp * 2 * half
     fresh = fresh_buf[...].reshape(n_fresh, dim)
-    for s in range(size):
-        vt_buf[:, s * cached : (s + 1) * cached] = v_buf[s].T
     vt_buf[:, size * cached :] = fresh.T
 
     key_row = lax.broadcasted_iota(jnp.int32, (n_fresh, 1), 0)
@@ -158,7 +174,7 @@
     first = cluster * size * cached
     cached_ok = first + lax.broadcasted_iota(jnp.int32, (size * cached, 1), 0) < hit
 
-    def chunk_step(turn, carry):
+    def score_chunk(turn, carry):
         chunk = lax.rem(blk // per_chunk + turn + 1, n_chunk)
         blocks = pl.ds(chunk * per_chunk, per_chunk)
         pltpu.make_async_copy(q_buf.at[blocks], q_buf.at[blocks], q_recv.at[chunk]).wait()
@@ -182,32 +198,29 @@
         p_new = jnp.exp2((s_new - top) * rate)
         weight = jnp.sum(p_old, axis=0, keepdims=True) + jnp.sum(p_new, axis=0, keepdims=True)
         p_new = pltpu.roll(p_new, half, 0)
-        nn = (((1,), (0,)), ((), ()))
-        mixed = lax.dot_general(
-            vt_buf[:, : size * cached], p_old.astype(jnp.bfloat16), nn,
-            preferred_element_type=jnp.float32,
-        ) + lax.dot_general(
-            vt_buf[:, size * cached :], p_new.astype(jnp.bfloat16), nn,
-            preferred_element_type=jnp.float32,
-        )
-        mixed = jnp.where(pos < count, mixed / jnp.maximum(weight, 1.0), 0.0)
+        p_buf[chunk, : size * cached] = p_old.astype(jnp.bfloat16)
+        p_buf[chunk, size * cached :] = p_new.astype(jnp.bfloat16)
+        w_buf[chunk] = jnp.where(pos < count, 1.0 / jnp.maximum(weight, 1.0), 0.0)
         level = top * rate + jnp.log2(jnp.maximum(weight, 1e-30))
+        for j in range(per_chunk):
+            l_own[chunk * per_chunk + j] = level[:, j * span : (j + 1) * span]
+        return carry
+
+    lax.fori_loop(0, n_chunk, score_chunk, 0)
+
+    for copy in v_copies:
+        copy.wait()
+    for s in range(size):
+        vt_buf[:, s * cached : (s + 1) * cached] = v_buf[s].T
+
+    def value_chunk(turn, carry):
+        chunk = lax.rem(blk // per_chunk + turn + 1, n_chunk)
+        blocks = pl.ds(chunk * per_chunk, per_chunk)
+        mixed = jnp.dot(vt_buf[...], p_buf[chunk], preferred_element_type=jnp.float32)
+        mixed = mixed * w_buf[chunk]
         n_dest = per_chunk * n_grp
         values = mixed.T.reshape(per_chunk, n_grp, rows, group, dim)
-        levels = jnp.broadcast_to(level, (dim, lanes)).T.reshape(n_dest, rows, group, dim)
-        spot = lax.broadcasted_iota(jnp.int32, (1, 1, dim), 2)
-        tile = jnp.zeros((n_dest, group, dim), jnp.float32)
-        for i in range(rows):
-            tile = jnp.where(spot % rows == i, levels[:, i], tile)
-        high = tile.astype(jnp.bfloat16).astype(jnp.float32)
-        middle = (tile - high).astype(jnp.bfloat16).astype(jnp.float32)
-        low = tile - high - middle
-        tile = jnp.where(spot < rows, high, jnp.where(spot < 2 * rows, middle, low))
-        tile = jnp.where(spot < 3 * rows, tile, 0.0)
-        o_buf[blocks, :, 0:rows] = values.astype(jnp.bfloat16)
-        o_buf[blocks, :, rows : rows + 1] = tile.astype(jnp.bfloat16).reshape(
-            per_chunk, n_grp, 1, group, dim
-        )
+        o_buf[blocks] = values.astype(jnp.bfloat16)
 
         def send_out(index, carry):
             to_blk = chunk * per_chunk + index // n_grp
@@ -217,6 +230,7 @@
             @pl.when(mine)
             def _():
                 pltpu.make_async_copy(o_buf.at[blk, grp], r_buf.at[blk, grp], o_recv).start()
+                pltpu.make_async_copy(l_own.at[blk], l_buf.at[blk, grp], l_recv).start()
 
             @pl.when(jnp.logical_not(mine))
             def _():
@@ -228,40 +242,44 @@
                     device_id={"blk": to_blk, "grp": to_grp},
                     device_id_type=MESH,
                 ).start()
+                pltpu.make_async_remote_copy(
+                    src_ref=l_own.at[to_blk],
+                    dst_ref=l_buf.at[blk, grp],
+                    send_sem=l_send,
+                    recv_sem=l_recv,
+                    device_id={"blk": to_blk, "grp": to_grp},
+                    device_id_type=MESH,
+                ).start()
 
             return carry
 
         lax.fori_loop(0, n_dest, send_out, 0)
         return carry
 
-    lax.fori_loop(0, n_chunk, chunk_step, 0)
-
+    lax.fori_loop(0, n_chunk, value_chunk, 0)
+
+    pltpu.make_async_copy(l_buf, l_buf, l_recv).wait()
+    levels = l_buf[...].reshape(n_cluster, size * n_grp, span)
+    scales = jnp.exp2(levels - jnp.max(levels, axis=0, keepdims=True))
+    scales = scales / jnp.sum(scales, axis=0, keepdims=True)
+    mine = pl.ds(pl.multiple_of(grp * rows * group, rows * group), rows * group)
+    shares = []
+    for c in range(n_cluster):
+        scale_buf[c] = scales[c].T
+        shares.append(scale_buf[c, mine, :])
     pltpu.make_async_copy(r_buf, r_buf, o_recv).wait()
-
-    def parts(c, h, r):
-        tile = r_buf[c * size + h, r, rows].astype(jnp.float32)
-        return tile + pltpu.roll(tile, dim - rows, 1) + pltpu.roll(tile, dim - 2 * rows, 1)
-
-    def finish(r, carry):
+    for r in range(requests):
         for h in range(size):
-            levels = [parts(c, h, r) for c in range(n_cluster)]
-            top = functools.reduce(jnp.maximum, levels)
-            scales = [jnp.exp2(level - top) for level in levels]
-            total = functools.reduce(jnp.add, scales)
-            scales = [scale / total for scale in scales]
-            for i in range(rows):
-                terms = [
-                    scales[c][:, i : i + 1] * r_buf[c * size + h, r, i].astype(jnp.float32)
-                    for c in range(n_cluster)
-                ]
-                out_ref[r, i, h * group : (h + 1) * group, :] = functools.reduce(
-                    jnp.add, terms
-                ).astype(out_ref.dtype)
-        return carry
-
-    lax.fori_loop(0, requests, finish, 0)
-
-    rest = n_dev - 1
+            column = slice(h * n_grp + r, h * n_grp + r + 1)
+            terms = [
+                shares[c][:, column].reshape(rows, group, 1)
+                * r_buf[c * size + h, r].astype(jnp.float32)
+                for c in range(n_cluster)
+            ]
+            joined = functools.reduce(jnp.add, terms).reshape(rows, group * dim)
+            cols = slice(h * group * dim, (h + 1) * group * dim)
+            out_ref[r, :, cols] = joined.astype(out_ref.dtype)
+
     q_flat = q_buf.at[0 : n_blk - 1]
     pltpu.make_async_copy(q_flat, q_flat, q_send).wait()
     q_flat = q_buf.at[0, 0 : n_grp - 1]
@@ -270,6 +288,10 @@
     pltpu.make_async_copy(r_flat, r_flat, o_send).wait()
     r_flat = r_buf.at[0, 0 : n_grp - 1]
     pltpu.make_async_copy(r_flat, r_flat, o_send).wait()
+    l_flat = l_buf.at[0 : n_blk - 1]
+    pltpu.make_async_copy(l_flat, l_flat, l_send).wait()
+    l_flat = l_buf.at[0, 0 : n_grp - 1]
+    pltpu.make_async_copy(l_flat, l_flat, l_send).wait()
     f_flat = fresh_buf.at[0 : size * n_grp - 1]
     pltpu.make_async_copy(f_flat, f_flat, fresh_send).wait()
 
@@ -285,6 +307,7 @@
         group = heads // size
         half = max(rows, 4)
         per_chunk = 2
+        span = rows * n_grp * group
         bf, f32 = jnp.bfloat16, jnp.float32
         vmem = pl.BlockSpec(memory_space=pltpu.VMEM)
         smem = pl.BlockSpec(memory_space=pltpu.SMEM)
@@ -292,10 +315,13 @@
         n_keys = size * cached + size * n_grp * 2 * half
         out = pl.pallas_call(
             functools.partial(kernel, n_blk, n_grp, size, per_chunk),
-            out_shape=jax.ShapeDtypeStruct((requests, rows, heads, HEAD_DIM), bf),
-            in_specs=[smem, smem, smem, vmem, vmem, vmem, hbm, hbm],
+            out_shape=jax.ShapeDtypeStruct((requests, rows, width), bf),
+            in_specs=[smem, smem, smem, hbm, hbm, hbm, hbm, hbm],
             out_specs=vmem,
             scratch_shapes=[
+                pltpu.VMEM(queries.shape, bf),
+                pltpu.VMEM(new_keys.shape, bf),
+                pltpu.VMEM(new_values.shape, bf),
                 pltpu.VMEM((requests, rows, heads, HEAD_DIM), bf),
                 pltpu.VMEM((cached, kv_width), bf),
                 pltpu.VMEM((cached, kv_width), bf),
@@ -305,16 +331,23 @@
                 pltpu.VMEM((requests, size, 2 * half, HEAD_DIM), bf),
                 pltpu.VMEM((size * n_grp, 2 * half, HEAD_DIM), bf),
                 pltpu.VMEM((n_blk, n_grp, rows, group, HEAD_DIM), bf),
-                pltpu.VMEM((n_blk, n_grp, rows + 1, group, HEAD_DIM), bf),
-                pltpu.VMEM((n_blk, n_grp, rows + 1, group, HEAD_DIM), bf),
+                pltpu.VMEM((n_blk, n_grp, rows, group, HEAD_DIM), bf),
+                pltpu.VMEM((n_blk, n_grp, rows, group, HEAD_DIM), bf),
+                pltpu.VMEM((n_blk // per_chunk, n_keys, per_chunk * span), bf),
+                pltpu.VMEM((n_blk // per_chunk, 1, per_chunk * span), f32),
+                pltpu.VMEM((n_blk, 1, span), f32),
+                pltpu.VMEM((n_blk, n_grp, 1, span), f32),
+                pltpu.VMEM((n_blk // size, span, size * n_grp), f32),
                 pltpu.SemaphoreType.REGULAR((2,)),
-                pltpu.SemaphoreType.DMA((2,)),
+                pltpu.SemaphoreType.DMA((5,)),
                 pltpu.SemaphoreType.DMA((size, 2)),
                 pltpu.SemaphoreType.DMA((size, 2)),
                 pltpu.SemaphoreType.DMA,
                 pltpu.SemaphoreType.DMA,
                 pltpu.SemaphoreType.DMA,
                 pltpu.SemaphoreType.DMA((n_blk // per_chunk,)),
+                pltpu.SemaphoreType.DMA,
+                pltpu.SemaphoreType.DMA,
                 pltpu.SemaphoreType.DMA,
                 pltpu.SemaphoreType.DMA,
             ],
@@ -325,7 +358,7 @@
             hits, counts, assign,
             queries, new_keys, new_values, cache_keys, cache_values,
         )
-        return out.reshape(requests, rows, width)
+        return out
 
     return jax.shard_map(
         local,

time: 37 us -> 33.9 us (0.916)
  Pallas kernels: 33.9 us -> 30.8 us
    pallas_call x1, Pallas kernels: 33.9 us -> 30.8 us  [local(): pl.pallas_call(functools.partial(kernel, n_blk, n_grp, size, per_chunk),...]
    unnamed x0 -> x1, local copies, waits for them, and re-layouts: none -> 1.61 us
    reshape x1 -> x0, local copies, waits for them, and re-layouts: 1.59 us -> none  [local(): return out.reshape(requests, rows, width)]
where the time goes in v3:
time: 33.9 us; the launch traced here: 33.7 us
  Pallas kernels  30.8 us (91%)
  local copies, waits for them, and re-layouts  1.61 us (5%)
  between operations  1.3 us (4%)
    pallas_call x1, Pallas kernels, local(): pl.pallas_call(functools.partial(kernel, n_blk, n_grp, size, per_chunk),...  30.8 us
    unnamed x1, local copies, waits for them, and re-layouts  1.61 us

profile of v3, /device:TPU:0, one launch (start us, length us, event | category | flops | bytes accessed | tf_op | source)
XLA Modules:
  0.0 33.7 jit_solution(2416696082344414845)
XLA Ops:
  1.3 30.8 %shard_map.82 = bf16[4,4,4096]{2,1,0:T(4,128)(2,1)} custom-call(s32[1]{0:T(128)S(6)} %copy.10.hits_ref, s32[1]{0:T(128)S(6)} %copy.11.counts_ref, s32[1,8]{1,0:T(1,128)} %assign_ref.1, bf16[4,4,4096]{2,1,0:T(4,128)(2,1)} %q_hbm.1, bf16[4,4,512]{2,1,0:T(4,128)(2,1)} %nk_hbm.1, bf16[4,4,512]{2,1,0:T(4,128)(2,1)} %nv_hbm.1, bf16[1,448,512]{2,1,0:T(8,128)(2,1)} %ck_ref.1, ...), custom_call_target="tpu_custom_call" | custom-call | tf_op jit(solution)/shard_map/pallas_call | solution.py:316
  32.1 1.6 %copy.12 = bf16[4,4,4096]{2,1,0:T(4,128)(2,1)} copy(bf16[4,4,4096]{2,1,0:T(4,128)(2,1)} %shard_map.82) | data formatting | bytes 262144
